TPU v7x, 32 devices: a whole 2x2x4 slice. The times are simulated.
32 devices in a mesh: gx: 16 (over z, y, core), gy: 2 (over x).
Axes of the slice: x: 2, y: 2, z: 4, core: 2. Of those that a mesh axis runs over, the one named last changes fastest.
Arguments:
- grid_field: bfloat16 [2, 256, 64, 512], P(None, 'gx', 'gy'), may hold values from -6 to 6
- spectral_weight: bfloat16 [128, 2, 512, 512], P('gx', None, None, 'gy'), may hold values from -0.1875 to 0.1875
- skip_weight: bfloat16 [512, 512], replicated, may hold values from -0.25 to 0.25
- inner_weight: bfloat16 [1024, 512], replicated, may hold values from -0.25 to 0.25
- outer_weight: bfloat16 [1024, 512], replicated, may hold values from -0.1875 to 0.1875
Outputs:
- layer_out: bfloat16 [2, 256, 64, 512], P(None, 'gx', 'gy')
All inputs are finite; a program needn't handle non-finite values.
Results may differ from a plain program's by a relative error of at most 0.0093.
Values may be sent and summed in bfloat16 or wider, within the bound.
No kernel may reach another device: no remote copies, remote signals or barrier semaphores. Data moves between devices by JAX's collectives and lax.ppermute only.
A program may use at most 64 MiB of HBM per device.

v0:
```python
import math
import jax
import jax.numpy as jnp
from jax import lax
from jax.sharding import PartitionSpec as P

KX = 16
KY = 8


def phase_table(row_ids, col_ids, total_rows, total_cols):
    x_modes = jnp.arange(KX, dtype=jnp.int32)
    y_modes = jnp.arange(KY, dtype=jnp.int32)
    x_phase = (x_modes[:, None] * row_ids[None, :] % total_rows).astype(jnp.float32) / total_rows
    y_phase = (y_modes[:, None] * col_ids[None, :] % total_cols).astype(jnp.float32) / total_cols
    angles = (x_phase[:, None, :, None] + y_phase[None, :, None, :]) * (2.0 * math.pi)
    angles = angles.reshape(KX * KY, row_ids.shape[0] * col_ids.shape[0])
    return jnp.concatenate([jnp.cos(angles), -jnp.sin(angles)], axis=0).astype(jnp.bfloat16)


def local(grid_field, spectral_weight, skip_weight, inner_weight, outer_weight):
    micro_count, row_count, col_count, width_count = grid_field.shape
    x_devices = lax.axis_size("gx")
    y_devices = lax.axis_size("gy")
    total_rows = row_count * x_devices
    total_cols = col_count * y_devices
    mode_count = KX * KY
    row_ids = lax.axis_index("gx") * row_count + jnp.arange(row_count, dtype=jnp.int32)
    col_ids = lax.axis_index("gy") * col_count + jnp.arange(col_count, dtype=jnp.int32)
    basis = phase_table(row_ids, col_ids, total_rows, total_cols)
    flat_rows = grid_field.reshape(micro_count, row_count * col_count, width_count)
    partial_value = jnp.einsum("kn,bnc->kbc", basis, flat_rows, preferred_element_type=jnp.float32)
    partial_value = partial_value.reshape(2, mode_count, micro_count, width_count)
    owned_modes = lax.psum_scatter(partial_value, "gx", scatter_dimension=1, tiled=True)
    owned_modes = lax.psum(owned_modes, "gy")
    spectrum = (owned_modes * (1.0 / math.sqrt(total_rows * total_cols))).astype(jnp.bfloat16)
    weight_re = spectral_weight[:, 0]
    weight_im = spectral_weight[:, 1]
    mixed_re = jnp.einsum(
        "mbc,mcd->mbd", spectrum[0], weight_re, preferred_element_type=jnp.float32
    ) - jnp.einsum("mbc,mcd->mbd", spectrum[1], weight_im, preferred_element_type=jnp.float32)
    mixed_im = jnp.einsum(
        "mbc,mcd->mbd", spectrum[0], weight_im, preferred_element_type=jnp.float32
    ) + jnp.einsum("mbc,mcd->mbd", spectrum[1], weight_re, preferred_element_type=jnp.float32)
    mixed_modes = jnp.stack([mixed_re, mixed_im]).astype(jnp.bfloat16)
    gathered = lax.all_gather(mixed_modes, "gy", axis=3, tiled=True)
    gathered = lax.all_gather(gathered, "gx", axis=1, tiled=True)
    gathered = gathered.reshape(2 * mode_count, micro_count, width_count)
    spectral = jnp.einsum("kn,kbc->bnc", basis, gathered, preferred_element_type=jnp.float32)
    spectral = spectral * (1.0 / math.sqrt(mode_count))
    skip_term = jnp.einsum(
        "bnc,cd->bnd", flat_rows, skip_weight, preferred_element_type=jnp.float32
    )
    active = jax.nn.gelu(spectral + skip_term).astype(jnp.bfloat16)
    hidden = jax.nn.gelu(
        jnp.einsum("bnc,hc->bnh", active, inner_weight, preferred_element_type=jnp.float32)
    )
    hidden = hidden.astype(jnp.bfloat16)
    feed_forward = jnp.einsum(
        "bnh,hc->bnc", hidden, outer_weight, preferred_element_type=jnp.float32
    )
    layer_out = (active.astype(jnp.float32) + feed_forward).astype(jnp.bfloat16)
    return layer_out.reshape(micro_count, row_count, col_count, width_count)


def solution(mesh):
    in_specs = (P(None, "gx", "gy", None), P("gx", None, None, "gy"), P(), P(), P())
    out_specs = P(None, "gx", "gy", None)
    return jax.shard_map(local, mesh=mesh, in_specs=in_specs, out_specs=out_specs, check_vma=False)
```

profile of v0, /device:TPU:0, one launch (start us, length us, event | category | flops | bytes accessed | tf_op | source)
XLA Modules:
  0.0 143.6 jit_solution(16070263595739132689)
XLA Ops:
  6.5 0.0 copy-start
  6.5 0.0 reduce-scatter.2.cloned.1.call-start
  6.6 4.1 %cosine_convert_fusion = (bf16[16,8,16,32]{3,2,1,0:T(8,128)(2,1)S(1)}, bf16[16,8,16,32]{3,2,1,0:T(8,128)(2,1)S(1)}) fusion(f32[8,32]{1,0:T(8,128)S(1)} %fusion.65, f32[16,16]{1,0:T(8,128)S(1)} %fusion.59), kind=kLoop, calls=%fused_computation.41 | loop fusion | flops 327680 | bytes 264192 | tf_op jit(solution)/shard_map/convert.7
  10.7 0.4 cos.7
  11.2 0.1 copy.14
  11.3 0.5 neg.7
  11.8 0.1 copy.15
  11.9 0.1 copy.16
  12.1 0.0 copy-done
  12.1 1.4 fusion.73
  13.5 0.0 reduce-scatter.2.cloned.1.call-update
  13.5 0.0 all-reduce.2.cloned.1.call-start
  13.6 60.4 %reduce-scatter.2.cloned.1.call-done = f32[2,8,2,512]{3,1,2,0:T(8,128)} async-done(((f32[2,128,2,512]{3,1,2,0:T(8,128)}), f32[2,8,2,512]{3,1,2,0:T(8,128)}) %reduce-scatter.2.cloned.1.call-update) | async-done | bytes 65552 | tf_op jit(solution)/shard_map/reduce_scatter | solution.py:34
  74.0 0.0 all-reduce.2.cloned.1.call-update
  74.0 1.7 %fusion.49 = f32[2,512,512]{2,1,0:T(8,128)S(1)} fusion(bf16[2,512,512]{2,1,0:T(8,128)(2,1)S(1)} %bitcast.69, bf16[512,512]{1,0:T(8,128)(2,1)} %param.7), kind=kOutput, calls=%fused_computation.43 | convolution fusion | flops 536870912 | bytes 3670016 | tf_op jit(solution)/shard_map/bnc,cd->bnd/dot_general | solution.py:51
  75.7 20.5 %all-reduce.2.cloned.1.call-done = f32[2,8,2,512]{3,1,2,0:T(8,128)} async-done(((f32[2,8,2,512]{3,1,2,0:T(8,128)}), f32[2,8,2,512]{3,1,2,0:T(8,128)}) %all-reduce.2.cloned.1.call-update) | async-done | bytes 65552 | tf_op jit(solution)/shard_map/psum | solution.py:35
  96.2 0.8 multiply_convert_fusion
  97.1 0.0 copy-start.1
  97.1 2.1 %fusion.18 = f32[8,2,256]{2,1,0:T(2,128)S(1)} fusion(bf16[8,2,512,256]{3,2,1,0:T(8,128)(2,1)} %param.6, bf16[8,2,512]{2,0,1:T(8,128)(2,1)S(1)} %get-tuple-element.5), kind=kOutput, calls=%fused_computation.20 | convolution fusion | flops 4194304 | bytes 2129920 | tf_op jit(solution)/shard_map/mbc,mcd->mbd/dot_general | solution.py:41
  99.2 2.0 %fusion.16 = f32[8,2,256]{2,1,0:T(2,128)S(1)} fusion(bf16[8,2,512,256]{3,2,1,0:T(8,128)(2,1)} %param.6, bf16[8,2,512]{2,0,1:T(8,128)(2,1)S(1)} %get-tuple-element.6), kind=kOutput, calls=%fused_computation.18 | convolution fusion | flops 4194304 | bytes 2129920 | tf_op jit(solution)/shard_map/mbc,mcd->mbd/dot_general | solution.py:42
  101.2 0.0 copy-done.1
  101.2 0.4 fusion.40
  101.6 0.4 fusion.43
  102.0 4.4 %all_gather.6 = bf16[2,8,2,512]{3,2,1,0:T(2,128)(2,1)S(1)} all-gather(bf16[2,8,2,256]{3,2,1,0:T(2,128)(2,1)S(1)} %pad_maximum_fusion.1), channel_id=1, replica_groups=mesh['gx'=16,'gy'=2] {'gy'}, dimensions={3}, use_global_device_ids=true | all-gather | bytes 49152 | tf_op jit(solution)/shard_map/all_gather | solution.py:46
  106.4 22.9 %all_gather.7 = bf16[2,128,2,512]{3,2,1,0:T(2,128)(2,1)S(1)} all-gather(bf16[2,8,2,512]{3,2,1,0:T(2,128)(2,1)S(1)} %all_gather.6), channel_id=1, replica_groups=mesh['gx'=16,'gy'=2] {'gx'}, dimensions={1}, use_global_device_ids=true | all-gather | bytes 557056 | tf_op jit(solution)/shard_map/all_gather | solution.py:47
  129.3 1.9 %fusion.15 = bf16[2,512,512]{2,1,0:T(8,128)(2,1)} fusion(f32[2,512,512]{2,1,0:T(8,128)S(1)} %fusion.49, bf16[256,2,512]{2,1,0:T(2,128)(2,1)S(1)} %bitcast.72, bf16[128,512]{0,1:T(8,128)(2,1)S(1)} %copy.15, bf16[128,512]{0,1:T(8,128)(2,1)S(1)} %copy.14), kind=kOutput, calls=%fused_computation.17 | convolution fusion | flops 274726912 | bytes 3932160 | tf_op jit(solution)/shard_map/kn,kbc->bnc/dot_general | solution.py:49
  131.2 5.5 %add_convert_fusion = bf16[2,512,512]{2,1,0:T(8,128)(2,1)} fusion(bf16[2,512,512]{2,1,0:T(8,128)(2,1)} %fusion.15, bf16[1024,512]{1,0:T(8,128)(2,1)} %param.9, bf16[1024,512]{1,0:T(8,128)(2,1)} %param.8), kind=kOutput, calls=%fused_computation.27 | convolution fusion | flops 2158493696 | bytes 4194304 | tf_op jit(solution)/shard_map/bnh,hc->bnc/dot_general | solution.py:59
  (7 shorter events, 0.1 us)
Async XLA Ops:
  6.5 5.5 %copy-start = (bf16[2,16,32,512]{3,2,1,0:T(8,128)(2,1)S(1)}, bf16[2,16,32,512]{3,2,1,0:T(8,128)(2,1)}, u32[]{:S(2)}) copy-start(bf16[2,16,32,512]{3,2,1,0:T(8,128)(2,1)} %param.5) | copy-start | bytes 3145732
  6.5 67.4 %reduce-scatter.2.cloned.1.call-start = ((), (), s32[]{:S(2)}) async-start(), calls=%async_computation.1 | async-start | bytes 1114112 | tf_op jit(solution)/shard_map/reduce_scatter | solution.py:34
  13.5 82.7 %all-reduce.2.cloned.1.call-start = ((), (), s32[]{:S(2)}) async-start(), calls=%async_computation.2 | async-start | bytes 131072 | tf_op jit(solution)/shard_map/psum | solution.py:35
  97.1 4.1 %copy-start.1 = (bf16[8,2,512,256]{3,2,1,0:T(8,128)(2,1)S(1)}, bf16[8,2,512,256]{3,2,1,0:T(8,128)(2,1)}, u32[]{:S(2)}) copy-start(bf16[8,2,512,256]{3,2,1,0:T(8,128)(2,1)} %param.6) | copy-start | bytes 12582916
Sparse Core Ops, SparseCore 0:
  13.6 60.2 reduce-scatter.1
  76.2 20.0 all-reduce.1
where the time goes:
time: 144 us
  waiting for transfers between devices  80.9 us (56%)
  blocking collectives  27.3 us (19%)
  matrix products  15.5 us (11%)
  between operations  13.5 us (9%)
  other arithmetic  5.08 us (4%)
    reduce_scatter x1, waiting for transfers between devices, local(): lax.psum_scatter(partial_value, 'gx', scatter_dimension=1, tiled=True)  60.4 us
    all_gather x1, blocking collectives, local(): gathered = lax.all_gather(gathered, 'gx', axis=1, tiled=True)  22.9 us
    psum x1, waiting for transfers between devices, local(): owned_modes = lax.psum(owned_modes, 'gy')  20.5 us
    dot_general x1, matrix products, local(): jnp.einsum('bnh,hc->bnc', hidden, outer_weight, preferred_element_type=jn...  5.53 us
    all_gather x1, blocking collectives, local(): gathered = lax.all_gather(mixed_modes, 'gy', axis=3, tiled=True)  4.41 us
    another operation x1, other arithmetic  4.14 us
  transfers between devices with their start and end apart: 2, of which 2 were waited for; matrix products, arithmetic and copies ran while one was open for 1% of the time, Pallas kernels for 0%

commit v1 on v0

--- a/solution.py
+++ b/solution.py
@@ -32,7 +32,7 @@
     partial_value = jnp.einsum("kn,bnc->kbc", basis, flat_rows, preferred_element_type=jnp.float32)
     partial_value = partial_value.reshape(2, mode_count, micro_count, width_count)
     owned_modes = lax.psum_scatter(partial_value, "gx", scatter_dimension=1, tiled=True)
-    owned_modes = lax.psum(owned_modes, "gy")
+    owned_modes = jnp.sum(lax.all_gather(owned_modes, "gy"), axis=0)
     spectrum = (owned_modes * (1.0 / math.sqrt(total_rows * total_cols))).astype(jnp.bfloat16)
     weight_re = spectral_weight[:, 0]
     weight_im = spectral_weight[:, 1]

time: 144 us -> 125 us (0.87)
  waiting for transfers between devices: 80.9 us -> 58.7 us
  blocking collectives: 27.3 us -> 30.4 us
    psum x1 -> x0, waiting for transfers between devices: 20.5 us -> none  [local(): owned_modes = lax.psum(owned_modes, 'gy')]
    all_gather x0 -> x1, blocking collectives: none -> 5.13 us  [local(): owned_modes = jnp.sum(lax.all_gather(owned_modes, 'gy'), axis=0)]
    all_gather x1, blocking collectives: 22.9 us -> 20.8 us  [local(): gathered = lax.all_gather(gathered, 'gx', axis=1, tiled=True)]
    reduce_scatter x1, waiting for transfers between devices: 60.4 us -> 58.7 us  [local(): lax.psum_scatter(partial_value, 'gx', scatter_dimension=1, tiled=True)]
  transfers between devices with their start and end apart: 2 -> 1, of which waited for: 2 -> 1; matrix products, arithmetic and copies ran while one was open for 1% -> 1% of each run, Pallas kernels for 0% -> 0%
where the time goes in v1:
time: 125 us
  waiting for transfers between devices  58.7 us (47%)
  blocking collectives  30.4 us (24%)
  matrix products  15.5 us (12%)
  between operations  13.5 us (11%)
  other arithmetic  5.72 us (5%)
  local copies, waits for them, and re-layouts  1.29 us (1%)
    reduce_scatter x1, waiting for transfers between devices, local(): lax.psum_scatter(partial_value, 'gx', scatter_dimension=1, tiled=True)  58.7 us
    all_gather x1, blocking collectives, local(): gathered = lax.all_gather(gathered, 'gx', axis=1, tiled=True)  20.8 us
    dot_general x1, matrix products, local(): jnp.einsum('bnh,hc->bnc', hidden, outer_weight, preferred_element_type=jn...  5.53 us
    all_gather x1, blocking collectives, local(): owned_modes = jnp.sum(lax.all_gather(owned_modes, 'gy'), axis=0)  5.13 us
    all_gather x1, blocking collectives, local(): gathered = lax.all_gather(mixed_modes, 'gy', axis=3, tiled=True)  4.41 us
    another operation x1, other arithmetic  4.14 us
  transfers between devices with their start and end apart: 1, of which 1 were waited for; matrix products, arithmetic and copies ran while one was open for 1% of the time, Pallas kernels for 0%

profile of v1, /device:TPU:0, one launch (start us, length us, event | category | flops | bytes accessed | tf_op | source)
XLA Modules:
  0.0 125.1 jit_solution(13347127083009650681)
XLA Ops:
  6.5 0.0 copy-start
  6.5 0.0 reduce-scatter.2.cloned.1.call-start
  6.6 4.1 %cosine_convert_fusion = (bf16[16,8,16,32]{3,2,1,0:T(8,128)(2,1)S(1)}, bf16[16,8,16,32]{3,2,1,0:T(8,128)(2,1)S(1)}) fusion(f32[8,32]{1,0:T(8,128)S(1)} %fusion.65, f32[16,16]{1,0:T(8,128)S(1)} %fusion.59), kind=kLoop, calls=%fused_computation.41 | loop fusion | flops 327680 | bytes 264192 | tf_op jit(solution)/shard_map/convert.7
  10.7 0.4 cos.7
  11.2 0.1 copy.23
  11.3 0.5 neg.7
  11.8 0.1 copy.24
  11.9 0.1 copy.25
  12.1 0.0 copy-done
  12.1 1.4 %fusion.73 = f32[2,128,2,512]{3,1,2,0:T(8,128)} fusion(bf16[2,128,512,1]{2,1,3,0:T(8,128)(2,1)S(1)} %bitcast.72, bf16[2,512,512,1]{2,1,0,3:T(8,128)(2,1)S(1)} %bitcast.71), kind=kOutput, calls=%fused_computation.80 | convolution fusion | flops 268435456 | bytes 2359296 | tf_op jit(solution)/shard_map/kn,bnc->kbc/dot_general | solution.py:32
  13.5 0.0 reduce-scatter.2.cloned.1.call-update
  13.5 1.7 %fusion.49 = f32[2,512,512]{2,1,0:T(8,128)S(1)} fusion(bf16[2,512,512]{2,1,0:T(8,128)(2,1)S(1)} %bitcast.70, bf16[512,512]{1,0:T(8,128)(2,1)} %param.7), kind=kOutput, calls=%fused_computation.43 | convolution fusion | flops 536870912 | bytes 3670016 | tf_op jit(solution)/shard_map/bnc,cd->bnd/dot_general | solution.py:51
  15.3 58.7 %reduce-scatter.2.cloned.1.call-done = f32[2,8,2,512]{3,1,2,0:T(8,128)} async-done(((f32[2,128,2,512]{3,1,2,0:T(8,128)}), f32[2,8,2,512]{3,1,2,0:T(8,128)}) %reduce-scatter.2.cloned.1.call-update) | async-done | bytes 65552 | tf_op jit(solution)/shard_map/reduce_scatter | solution.py:34
  74.0 5.1 %all-gather = f32[4,8,2,512]{3,1,2,0:T(8,128)S(1)} all-gather(f32[2,8,2,512]{3,1,2,0:T(8,128)} %reduce-scatter.2.cloned.1.call-done), channel_id=2, replica_groups=mesh['gx'=16,'gy'=2] {'gy'}, dimensions={0}, use_global_device_ids=true | all-gather | bytes 196608 | tf_op jit(solution)/shard_map/all_gather | solution.py:35
  79.1 0.6 reduce_sum.9
  79.7 0.8 multiply_convert_fusion
  80.6 0.0 copy-start.1
  80.6 2.1 %fusion.18 = f32[8,2,256]{2,1,0:T(2,128)S(1)} fusion(bf16[8,2,512,256]{3,2,1,0:T(8,128)(2,1)} %param.6, bf16[8,2,512]{2,0,1:T(8,128)(2,1)S(1)} %get-tuple-element.5), kind=kOutput, calls=%fused_computation.20 | convolution fusion | flops 4194304 | bytes 2129920 | tf_op jit(solution)/shard_map/mbc,mcd->mbd/dot_general | solution.py:41
  82.7 2.0 %fusion.16 = f32[8,2,256]{2,1,0:T(2,128)S(1)} fusion(bf16[8,2,512,256]{3,2,1,0:T(8,128)(2,1)} %param.6, bf16[8,2,512]{2,0,1:T(8,128)(2,1)S(1)} %get-tuple-element.6), kind=kOutput, calls=%fused_computation.18 | convolution fusion | flops 4194304 | bytes 2129920 | tf_op jit(solution)/shard_map/mbc,mcd->mbd/dot_general | solution.py:42
  84.7 0.0 copy-done.1
  84.7 0.4 fusion.40
  85.1 0.4 fusion.43
  85.5 4.4 %all_gather.14 = bf16[2,8,2,512]{3,2,1,0:T(2,128)(2,1)S(1)} all-gather(bf16[2,8,2,256]{3,2,1,0:T(2,128)(2,1)S(1)} %pad_maximum_fusion.1), channel_id=1, replica_groups=mesh['gx'=16,'gy'=2] {'gy'}, dimensions={3}, use_global_device_ids=true | all-gather | bytes 49152 | tf_op jit(solution)/shard_map/all_gather | solution.py:46
  89.9 20.8 %all_gather.15 = bf16[2,128,2,512]{3,2,1,0:T(2,128)(2,1)S(1)} all-gather(bf16[2,8,2,512]{3,2,1,0:T(2,128)(2,1)S(1)} %all_gather.14), channel_id=1, replica_groups=mesh['gx'=16,'gy'=2] {'gx'}, dimensions={1}, use_global_device_ids=true | all-gather | bytes 557056 | tf_op jit(solution)/shard_map/all_gather | solution.py:47
  110.8 1.9 %fusion.15 = bf16[2,512,512]{2,1,0:T(8,128)(2,1)} fusion(f32[2,512,512]{2,1,0:T(8,128)S(1)} %fusion.49, bf16[256,2,512]{2,1,0:T(2,128)(2,1)S(1)} %bitcast.74, bf16[128,512]{0,1:T(8,128)(2,1)S(1)} %copy.24, bf16[128,512]{0,1:T(8,128)(2,1)S(1)} %copy.23), kind=kOutput, calls=%fused_computation.17 | convolution fusion | flops 274726912 | bytes 3932160 | tf_op jit(solution)/shard_map/kn,kbc->bnc/dot_general | solution.py:49
  112.7 5.5 %add_convert_fusion = bf16[2,512,512]{2,1,0:T(8,128)(2,1)} fusion(bf16[2,512,512]{2,1,0:T(8,128)(2,1)} %fusion.15, bf16[1024,512]{1,0:T(8,128)(2,1)} %param.9, bf16[1024,512]{1,0:T(8,128)(2,1)} %param.8), kind=kOutput, calls=%fused_computation.27 | convolution fusion | flops 2158493696 | bytes 4194304 | tf_op jit(solution)/shard_map/bnh,hc->bnc/dot_general | solution.py:59
  (7 shorter events, 0.1 us)
Async XLA Ops:
  6.5 5.5 %copy-start = (bf16[2,16,32,512]{3,2,1,0:T(8,128)(2,1)S(1)}, bf16[2,16,32,512]{3,2,1,0:T(8,128)(2,1)}, u32[]{:S(2)}) copy-start(bf16[2,16,32,512]{3,2,1,0:T(8,128)(2,1)} %param.5) | copy-start | bytes 3145732
  6.5 67.4 %reduce-scatter.2.cloned.1.call-start = ((), (), s32[]{:S(2)}) async-start(), calls=%async_computation.1 | async-start | bytes 1114112 | tf_op jit(solution)/shard_map/reduce_scatter | solution.py:34
  80.6 4.1 %copy-start.1 = (bf16[8,2,512,256]{3,2,1,0:T(8,128)(2,1)S(1)}, bf16[8,2,512,256]{3,2,1,0:T(8,128)(2,1)}, u32[]{:S(2)}) copy-start(bf16[8,2,512,256]{3,2,1,0:T(8,128)(2,1)} %param.6) | copy-start | bytes 12582916
Sparse Core Ops, SparseCore 0:
  13.6 60.2 reduce-scatter.1

commit v2 on v0

--- a/solution.py
+++ b/solution.py
@@ -44,7 +44,7 @@
     ) + jnp.einsum("mbc,mcd->mbd", spectrum[1], weight_re, preferred_element_type=jnp.float32)
     mixed_modes = jnp.stack([mixed_re, mixed_im]).astype(jnp.bfloat16)
     gathered = lax.all_gather(mixed_modes, "gy", axis=3, tiled=True)
-    gathered = lax.all_gather(gathered, "gx", axis=1, tiled=True)
+    gathered = jnp.concatenate(lax.all_gather(gathered, "gx"), axis=1)
     gathered = gathered.reshape(2 * mode_count, micro_count, width_count)
     spectral = jnp.einsum("kn,kbc->bnc", basis, gathered, preferred_element_type=jnp.float32)
     spectral = spectral * (1.0 / math.sqrt(mode_count))

time: 144 us -> 144 us (level)
  no operation moved by 1% of the time
where the time goes in v2:
time: 144 us
  waiting for transfers between devices  80.9 us (56%)
  blocking collectives  27.3 us (19%)
  matrix products  15.5 us (11%)
  between operations  13.5 us (9%)
  other arithmetic  5.08 us (4%)
    reduce_scatter x1, waiting for transfers between devices, local(): lax.psum_scatter(partial_value, 'gx', scatter_dimension=1, tiled=True)  60.4 us
    all_gather x1, blocking collectives, local(): gathered = jnp.concatenate(lax.all_gather(gathered, 'gx'), axis=1)  22.9 us
    psum x1, waiting for transfers between devices, local(): owned_modes = lax.psum(owned_modes, 'gy')  20.5 us
    dot_general x1, matrix products, local(): jnp.einsum('bnh,hc->bnc', hidden, outer_weight, preferred_element_type=jn...  5.53 us
    all_gather x1, blocking collectives, local(): gathered = lax.all_gather(mixed_modes, 'gy', axis=3, tiled=True)  4.41 us
    another operation x1, other arithmetic  4.14 us
  transfers between devices with their start and end apart: 2, of which 2 were waited for; matrix products, arithmetic and copies ran while one was open for 1% of the time, Pallas kernels for 0%

profile of v2, /device:TPU:0, one launch (start us, length us, event | category | flops | bytes accessed | tf_op | source)
XLA Modules:
  0.0 143.7 jit_solution(4513634466796870950)
XLA Ops:
  6.5 0.0 copy-start
  6.5 0.0 reduce-scatter.2.cloned.1.call-start
  6.6 4.1 %cosine_convert_fusion = (bf16[16,8,16,32]{3,2,1,0:T(8,128)(2,1)S(1)}, bf16[16,8,16,32]{3,2,1,0:T(8,128)(2,1)S(1)}) fusion(f32[8,32]{1,0:T(8,128)S(1)} %fusion.64, f32[16,16]{1,0:T(8,128)S(1)} %fusion.58), kind=kLoop, calls=%fused_computation.41 | loop fusion | flops 327680 | bytes 264192 | tf_op jit(solution)/shard_map/convert.7
  10.7 0.4 cos.7
  11.2 0.1 copy.24
  11.3 0.5 neg.7
  11.8 0.1 copy.25
  11.9 0.1 copy.26
  12.1 0.0 copy-done
  12.1 1.4 fusion.72
  13.5 0.0 reduce-scatter.2.cloned.1.call-update
  13.5 0.0 all-reduce.2.cloned.1.call-start
  13.6 60.4 %reduce-scatter.2.cloned.1.call-done = f32[2,8,2,512]{3,1,2,0:T(8,128)} async-done(((f32[2,128,2,512]{3,1,2,0:T(8,128)}), f32[2,8,2,512]{3,1,2,0:T(8,128)}) %reduce-scatter.2.cloned.1.call-update) | async-done | bytes 65552 | tf_op jit(solution)/shard_map/reduce_scatter | solution.py:34
  74.0 0.0 all-reduce.2.cloned.1.call-update
  74.0 1.7 %fusion.49 = f32[2,512,512]{2,1,0:T(8,128)S(1)} fusion(bf16[2,512,512]{2,1,0:T(8,128)(2,1)S(1)} %bitcast.73, bf16[512,512]{1,0:T(8,128)(2,1)} %param.7), kind=kOutput, calls=%fused_computation.43 | convolution fusion | flops 536870912 | bytes 3670016 | tf_op jit(solution)/shard_map/bnc,cd->bnd/dot_general | solution.py:51
  75.7 20.5 %all-reduce.2.cloned.1.call-done = f32[2,8,2,512]{3,1,2,0:T(8,128)} async-done(((f32[2,8,2,512]{3,1,2,0:T(8,128)}), f32[2,8,2,512]{3,1,2,0:T(8,128)}) %all-reduce.2.cloned.1.call-update) | async-done | bytes 65552 | tf_op jit(solution)/shard_map/psum | solution.py:35
  96.2 0.8 multiply_convert_fusion
  97.1 0.0 copy-start.1
  97.1 2.1 %fusion.18 = f32[8,2,256]{2,1,0:T(2,128)S(1)} fusion(bf16[8,2,512,256]{3,2,1,0:T(8,128)(2,1)} %param.6, bf16[8,2,512]{2,0,1:T(8,128)(2,1)S(1)} %get-tuple-element.5), kind=kOutput, calls=%fused_computation.20 | convolution fusion | flops 4194304 | bytes 2129920 | tf_op jit(solution)/shard_map/mbc,mcd->mbd/dot_general | solution.py:41
  99.2 2.0 %fusion.16 = f32[8,2,256]{2,1,0:T(2,128)S(1)} fusion(bf16[8,2,512,256]{3,2,1,0:T(8,128)(2,1)} %param.6, bf16[8,2,512]{2,0,1:T(8,128)(2,1)S(1)} %get-tuple-element.6), kind=kOutput, calls=%fused_computation.18 | convolution fusion | flops 4194304 | bytes 2129920 | tf_op jit(solution)/shard_map/mbc,mcd->mbd/dot_general | solution.py:42
  101.2 0.0 copy-done.1
  101.2 0.4 fusion.40
  101.6 0.4 fusion.43
  102.0 4.4 %all_gather.9 = bf16[2,8,2,512]{3,2,1,0:T(2,128)(2,1)S(1)} all-gather(bf16[2,8,2,256]{3,2,1,0:T(2,128)(2,1)S(1)} %pad_maximum_fusion.1), channel_id=1, replica_groups=mesh['gx'=16,'gy'=2] {'gy'}, dimensions={3}, use_global_device_ids=true | all-gather | bytes 49152 | tf_op jit(solution)/shard_map/all_gather | solution.py:46
  106.4 22.9 %all-gather = bf16[32,8,2,512]{3,1,2,0:T(8,128)(2,1)S(1)} all-gather(bf16[2,8,2,512]{3,1,2,0:T(8,128)(2,1)S(1)} %copy.33), channel_id=2, replica_groups=mesh['gx'=16,'gy'=2] {'gx'}, dimensions={0}, use_global_device_ids=true | all-gather | bytes 557056 | tf_op jit(solution)/shard_map/all_gather | solution.py:47
  129.4 1.9 %fusion.15 = bf16[2,512,512]{2,1,0:T(8,128)(2,1)} fusion(f32[2,512,512]{2,1,0:T(8,128)S(1)} %fusion.49, bf16[256,2,512]{2,0,1:T(8,128)(2,1)S(1)} %bitcast.77, bf16[128,512]{0,1:T(8,128)(2,1)S(1)} %copy.25, bf16[128,512]{0,1:T(8,128)(2,1)S(1)} %copy.24), kind=kOutput, calls=%fused_computation.17 | convolution fusion | flops 274726912 | bytes 3932160 | tf_op jit(solution)/shard_map/kn,kbc->bnc/dot_general | solution.py:49
  131.3 5.5 %add_convert_fusion = bf16[2,512,512]{2,1,0:T(8,128)(2,1)} fusion(bf16[2,512,512]{2,1,0:T(8,128)(2,1)} %fusion.15, bf16[1024,512]{1,0:T(8,128)(2,1)} %param.9, bf16[1024,512]{1,0:T(8,128)(2,1)} %param.8), kind=kOutput, calls=%fused_computation.27 | convolution fusion | flops 2158493696 | bytes 4194304 | tf_op jit(solution)/shard_map/bnh,hc->bnc/dot_general | solution.py:59
  (9 shorter events, 0.1 us)
Async XLA Ops:
  6.5 5.5 %copy-start = (bf16[2,16,32,512]{3,2,1,0:T(8,128)(2,1)S(1)}, bf16[2,16,32,512]{3,2,1,0:T(8,128)(2,1)}, u32[]{:S(2)}) copy-start(bf16[2,16,32,512]{3,2,1,0:T(8,128)(2,1)} %param.5) | copy-start | bytes 3145732
  6.5 67.4 %reduce-scatter.2.cloned.1.call-start = ((), (), s32[]{:S(2)}) async-start(), calls=%async_computation.1 | async-start | bytes 1114112 | tf_op jit(solution)/shard_map/reduce_scatter | solution.py:34
  13.5 82.7 %all-reduce.2.cloned.1.call-start = ((), (), s32[]{:S(2)}) async-start(), calls=%async_computation.2 | async-start | bytes 131072 | tf_op jit(solution)/shard_map/psum | solution.py:35
  97.1 4.1 %copy-start.1 = (bf16[8,2,512,256]{3,2,1,0:T(8,128)(2,1)S(1)}, bf16[8,2,512,256]{3,2,1,0:T(8,128)(2,1)}, u32[]{:S(2)}) copy-start(bf16[8,2,512,256]{3,2,1,0:T(8,128)(2,1)} %param.6) | copy-start | bytes 12582916
Sparse Core Ops, SparseCore 0:
  13.6 60.2 reduce-scatter.1
  76.2 20.0 all-reduce.1
